TPU v7x, 32 devices: a whole 2x2x4 slice. The times are simulated.
32 devices in a mesh: row: 4 (over x, core), col: 2 (over y), dp: 4 (over z).
Axes of the slice: x: 2, y: 2, z: 4, core: 2. Of those that a mesh axis runs over, the one named last changes fastest.
Arguments:
- tokens: bfloat16 [16384, 768], P(('dp', 'col', 'row')), may hold values from -6 to 6
- encoded: bfloat16 [12000, 768], P(('dp', 'col', 'row')), may hold values from -6 to 6
- branch: int32 [8, 4], P(('dp', 'col')), may hold values from 512 to 1024
- cotangent: bfloat16 [16384, 768], P(('dp', 'col', 'row')), may hold values from -6 to 6
- gain_self: float32 [768], replicated, may hold values from 0.5 to 1.5
- self_query: bfloat16 [768, 768], P('col', 'row'), may hold values from -0.21875 to 0.21875
- self_key: bfloat16 [768, 768], P('col', 'row'), may hold values from -0.21875 to 0.21875
- self_value: bfloat16 [768, 768], P('col', 'row'), may hold values from -0.21875 to 0.21875
- self_out: bfloat16 [768, 768], P('row', 'col'), may hold values from -3 to 3
- gain_cross: float32 [768], replicated, may hold values from 0.5 to 1.5
- cross_query: bfloat16 [768, 768], P('col', 'row'), may hold values from -0.21875 to 0.21875
- cross_key: bfloat16 [768, 768], P('col', 'row'), may hold values from -0.21875 to 0.21875
- cross_value: bfloat16 [768, 768], P('col', 'row'), may hold values from -0.21875 to 0.21875
- cross_out: bfloat16 [768, 768], P('row', 'col'), may hold values from -4 to 4
- gain_hidden: float32 [768], replicated, may hold values from 0.5 to 1.5
- hidden_up: bfloat16 [768, 3072], P('col', 'row'), may hold values from -0.21875 to 0.21875
- hidden_down: bfloat16 [3072, 768], P('row', 'col'), may hold values from -0.109375 to 0.109375
- gain_final: float32 [768], replicated, may hold values from 0.5 to 1.5
Outputs:
- layer_out: bfloat16 [16384, 768], P(('dp', 'col', 'row'))
- grad_tokens: float32 [16384, 768], P(('dp', 'col', 'row'))
- grad_encoded: float32 [12000, 768], P(('dp', 'col', 'row'))
- grad_gain_self: float32 [768], replicated
- grad_self_query: float32 [768, 768], P('col', 'row')
- grad_self_key: float32 [768, 768], P('col', 'row')
- grad_self_value: float32 [768, 768], P('col', 'row')
- grad_self_out: float32 [768, 768], P('row', 'col')
- grad_gain_cross: float32 [768], replicated
- grad_cross_query: float32 [768, 768], P('col', 'row')
- grad_cross_key: float32 [768, 768], P('col', 'row')
- grad_cross_value: float32 [768, 768], P('col', 'row')
- grad_cross_out: float32 [768, 768], P('row', 'col')
- grad_gain_hidden: float32 [768], replicated
- grad_hidden_up: float32 [768, 3072], P('col', 'row')
- grad_hidden_down: float32 [3072, 768], P('row', 'col')
- grad_gain_final: float32 [768], replicated
Inputs may be any that keep to these rules, and one draw needn't show every extreme that they name: Continuation j of family f sees the first branch[f, j] prompt positions.
All inputs are finite; a program needn't handle non-finite values.
Results may differ from a plain program's by a relative error of at most 0.025.
Values may be sent and summed in bfloat16 or wider, within the bound.
A program may use at most 192 MiB of HBM per device.

v0:
```python
import jax
import jax.numpy as jnp
from jax import lax
from jax.sharding import PartitionSpec as P

HEAD_DIM = 64
PROMPT = 1024
CONT = 256
NCONT = 4
eps = 1e-05
big_neg = -1e30


def matmul(left, right):
    return jnp.dot(left, right, preferred_element_type=jnp.float32)


def inner_left(left, right):
    return lax.dot_general(
        left, right, (((0,), (0,)), ((), ())), preferred_element_type=jnp.float32
    )


def inner_right(left, right):
    return lax.dot_general(
        left, right, (((1,), (1,)), ((), ())), preferred_element_type=jnp.float32
    )


def unit_rows(rows_in):
    average = jnp.mean(rows_in, axis=-1, keepdims=True)
    centred = rows_in - average
    variance = jnp.mean(centred * centred, axis=-1, keepdims=True)
    return centred * lax.rsqrt(variance + eps)


def norm_back(rows_in, gain, upstream):
    outcome, pullback = jax.vjp(lambda values_in: unit_rows(values_in) * gain, rows_in)
    return pullback(upstream)[0]


def visible(query_pos, key_pos, branch_row):
    query_at = query_pos[:, None]
    key_at = key_pos[None, :]
    query_cont = (query_at - PROMPT) // CONT
    key_cont = (key_at - PROMPT) // CONT
    chosen = (query_cont == jnp.arange(NCONT, dtype=jnp.int32)[None, :]).astype(jnp.int32)
    limit = jnp.sum(chosen * branch_row[None, :], axis=1, keepdims=True)
    same_cont = (key_cont == query_cont) & (key_at <= query_at)
    return jnp.where(
        query_at < PROMPT, key_at <= query_at, jnp.where(key_at < PROMPT, key_at < limit, same_cont)
    )


def block_scores(piece, split_k, anchor, key_pos, branch_row, scaling):
    scores = (
        jnp.einsum("qhd,khd->hqk", piece, split_k, preferred_element_type=jnp.float32) * scaling
    )
    if branch_row is not None:
        shown = visible(anchor + jnp.arange(piece.shape[0], dtype=jnp.int32), key_pos, branch_row)
        scores = jnp.where(shown[None], scores, big_neg)
    return scores


def attend(queries, key_rows, value_rows, branch_row):
    length = queries.shape[0]
    features = queries.shape[1]
    head_count = features // HEAD_DIM
    block_rows = min(512, length)
    blocks = length // block_rows
    scaling = HEAD_DIM ** (-0.5)
    split_q = queries.reshape(blocks, block_rows, head_count, HEAD_DIM)
    split_k = key_rows.reshape(key_rows.shape[0], head_count, HEAD_DIM)
    split_v = value_rows.reshape(value_rows.shape[0], head_count, HEAD_DIM)
    key_pos = jnp.arange(key_rows.shape[0], dtype=jnp.int32)

    def one_block(inputs):
        piece, anchor = inputs
        scores = block_scores(piece, split_k, anchor, key_pos, branch_row, scaling)
        highest = jnp.max(scores, axis=-1, keepdims=True)
        raised = jnp.exp(scores - highest)
        denominator = jnp.sum(raised, axis=-1, keepdims=True)
        weights = (raised / denominator).astype(jnp.bfloat16)
        blended = jnp.einsum("hqk,khd->qhd", weights, split_v, preferred_element_type=jnp.float32)
        return (
            blended.reshape(block_rows, features).astype(jnp.bfloat16),
            (highest + jnp.log(denominator))[..., 0],
        )

    starts = jnp.arange(blocks, dtype=jnp.int32) * block_rows
    blended, logsum = lax.map(one_block, (split_q, starts))
    return (blended.reshape(length, features), logsum)


def attend_back(queries, key_rows, value_rows, grad_blended, logsum, branch_row):
    length = queries.shape[0]
    features = queries.shape[1]
    head_count = features // HEAD_DIM
    block_rows = min(512, length)
    blocks = length // block_rows
    scaling = HEAD_DIM ** (-0.5)
    split_q = queries.reshape(blocks, block_rows, head_count, HEAD_DIM)
    split_g = grad_blended.reshape(blocks, block_rows, head_count, HEAD_DIM)
    split_k = key_rows.reshape(key_rows.shape[0], head_count, HEAD_DIM)
    split_v = value_rows.reshape(value_rows.shape[0], head_count, HEAD_DIM)
    key_pos = jnp.arange(key_rows.shape[0], dtype=jnp.int32)

    def one_block(running, inputs):
        piece, grad_piece, anchor, block_sum = inputs
        scores = block_scores(piece, split_k, anchor, key_pos, branch_row, scaling)
        weights = jnp.exp(scores - block_sum[..., None])
        rounded = weights.astype(jnp.bfloat16)
        through = jnp.einsum(
            "qhd,khd->hqk", grad_piece, split_v, preferred_element_type=jnp.float32
        )
        centre = jnp.sum(weights * through, axis=-1, keepdims=True)
        sloped = (weights * (through - centre)).astype(jnp.bfloat16)
        grad_query = (
            jnp.einsum("hqk,khd->qhd", sloped, split_k, preferred_element_type=jnp.float32)
            * scaling
        )
        grad_keys = (
            running[0]
            + jnp.einsum("hqk,qhd->khd", sloped, piece, preferred_element_type=jnp.float32)
            * scaling
        )
        grad_values = running[1] + jnp.einsum(
            "hqk,qhd->khd", rounded, grad_piece, preferred_element_type=jnp.float32
        )
        return ((grad_keys, grad_values), grad_query.reshape(block_rows, features))

    blank_keys = jnp.zeros((key_rows.shape[0], head_count, HEAD_DIM), jnp.float32)
    starts = jnp.arange(blocks, dtype=jnp.int32) * block_rows
    (grad_keys, grad_values), grad_query = lax.scan(
        one_block, (blank_keys, blank_keys), (split_q, split_g, starts, logsum)
    )
    return (
        grad_query.reshape(length, features).astype(jnp.bfloat16),
        grad_keys.reshape(-1, features).astype(jnp.bfloat16),
        grad_values.reshape(-1, features).astype(jnp.bfloat16),
    )


def local(
    tokens,
    encoded,
    branch,
    cotangent,
    gain_self,
    self_query,
    self_key,
    self_value,
    self_out,
    gain_cross,
    cross_query,
    cross_key,
    cross_value,
    cross_out,
    gain_hidden,
    hidden_up,
    hidden_down,
    gain_final,
):
    local_rows = tokens.shape[0]
    offset = lax.axis_index("row") * local_rows
    branch_row = branch[0]

    def spread(piece):
        return lax.all_gather(piece, "row", axis=0, tiled=True)

    def own_slice(value):
        return lax.dynamic_slice_in_dim(value, offset, local_rows, 0)

    def scatter_rows(parts, apply):
        return lax.psum_scatter(
            apply(tuple((piece for piece in parts))).astype(jnp.bfloat16),
            "row",
            scatter_dimension=0,
            tiled=True,
        ).astype(jnp.float32)

    def settle(parts, apply):
        return lax.psum(apply(parts), "row")

    def gain_term(upstream, rows_in):
        return jnp.sum(own_slice(upstream) * unit_rows(own_slice(rows_in)), axis=0)

    full_query, full_key, full_value, full_cquery, full_ckey, full_cvalue, full_up = (
        lax.all_gather(self_query, "col", axis=0, tiled=True),
        lax.all_gather(self_key, "col", axis=0, tiled=True),
        lax.all_gather(self_value, "col", axis=0, tiled=True),
        lax.all_gather(cross_query, "col", axis=0, tiled=True),
        lax.all_gather(cross_key, "col", axis=0, tiled=True),
        lax.all_gather(cross_value, "col", axis=0, tiled=True),
        lax.all_gather(hidden_up, "col", axis=0, tiled=True),
    )
    full_out, full_cout, full_down = (
        lax.all_gather(self_out, "col", axis=1, tiled=True),
        lax.all_gather(cross_out, "col", axis=1, tiled=True),
        lax.all_gather(hidden_down, "col", axis=1, tiled=True),
    )
    frames = spread(encoded)
    residual = spread(tokens).astype(jnp.float32)
    wide_self = (unit_rows(residual) * gain_self).astype(jnp.bfloat16)
    queries = matmul(wide_self, full_query).astype(jnp.bfloat16)
    key_rows = matmul(wide_self, full_key).astype(jnp.bfloat16)
    value_rows = matmul(wide_self, full_value).astype(jnp.bfloat16)
    blended_self, logsum_self = attend(queries, key_rows, value_rows, branch_row)
    after_self = residual + settle((blended_self,), lambda parts: matmul(parts[0], full_out))
    wide_cross = (unit_rows(after_self) * gain_cross).astype(jnp.bfloat16)
    cross_queries = matmul(wide_cross, full_cquery).astype(jnp.bfloat16)
    cross_keys = matmul(frames, full_ckey).astype(jnp.bfloat16)
    cross_values = matmul(frames, full_cvalue).astype(jnp.bfloat16)
    blended_cross, logsum_cross = attend(cross_queries, cross_keys, cross_values, None)
    after_cross = after_self + settle((blended_cross,), lambda parts: matmul(parts[0], full_cout))
    wide_hidden = (unit_rows(after_cross) * gain_hidden).astype(jnp.bfloat16)
    raised = matmul(wide_hidden, full_up)
    active = jax.nn.gelu(raised, approximate=False).astype(jnp.bfloat16)
    after_hidden = after_cross + settle((active,), lambda parts: matmul(parts[0], full_down))
    layer_out = own_slice(unit_rows(after_hidden) * gain_final).astype(jnp.bfloat16)
    upstream = spread(cotangent).astype(jnp.float32)
    final_gain = gain_term(upstream, after_hidden)
    grad_hidden = norm_back(after_hidden, gain_final, upstream)
    sent_hidden = grad_hidden.astype(jnp.bfloat16)
    grad_down = inner_left(active, sent_hidden)
    outcome, gelu_pull = jax.vjp(
        lambda values_in: jax.nn.gelu(values_in, approximate=False), raised
    )
    grad_raised = gelu_pull(inner_right(sent_hidden, full_down))[0].astype(jnp.bfloat16)
    grad_up = inner_left(wide_hidden, grad_raised)
    grad_normed = settle((grad_raised,), lambda parts: inner_right(parts[0], full_up))
    hidden_gain = gain_term(grad_normed, after_cross)
    grad_cross = grad_hidden + norm_back(after_cross, gain_hidden, grad_normed)
    sent_cross = grad_cross.astype(jnp.bfloat16)
    grad_cout = inner_left(blended_cross, sent_cross)
    grad_blended = inner_right(sent_cross, full_cout).astype(jnp.bfloat16)
    grad_cq, grad_ck, grad_cv = attend_back(
        cross_queries, cross_keys, cross_values, grad_blended, logsum_cross, None
    )
    grad_cquery = inner_left(wide_cross, grad_cq)
    grad_ckey = inner_left(frames, grad_ck)
    grad_cvalue = inner_left(frames, grad_cv)
    grad_encoded = scatter_rows(
        (grad_ck, grad_cv),
        lambda parts: inner_right(parts[0], full_ckey) + inner_right(parts[1], full_cvalue),
    )
    grad_normed = settle((grad_cq,), lambda parts: inner_right(parts[0], full_cquery))
    cross_gain = gain_term(grad_normed, after_self)
    grad_self = grad_cross + norm_back(after_self, gain_cross, grad_normed)
    sent_self = grad_self.astype(jnp.bfloat16)
    grad_out = inner_left(blended_self, sent_self)
    grad_blended = inner_right(sent_self, full_out).astype(jnp.bfloat16)
    grad_qs, grad_ks, grad_vs = attend_back(
        queries, key_rows, value_rows, grad_blended, logsum_self, branch_row
    )
    grad_query = inner_left(wide_self, grad_qs)
    grad_key = inner_left(wide_self, grad_ks)
    grad_value = inner_left(wide_self, grad_vs)
    grad_normed = settle(
        (grad_qs, grad_ks, grad_vs),
        lambda parts: inner_right(parts[0], full_query)
        + inner_right(parts[1], full_key)
        + inner_right(parts[2], full_value),
    )
    self_gain = gain_term(grad_normed, residual)
    grad_tokens = own_slice(grad_self + norm_back(residual, gain_self, grad_normed))
    grad_query, grad_key, grad_value, grad_cquery, grad_ckey, grad_cvalue, grad_up = (
        lax.psum_scatter(
            grad_query.astype(jnp.bfloat16), "col", scatter_dimension=0, tiled=True
        ).astype(jnp.float32),
        lax.psum_scatter(
            grad_key.astype(jnp.bfloat16), "col", scatter_dimension=0, tiled=True
        ).astype(jnp.float32),
        lax.psum_scatter(
            grad_value.astype(jnp.bfloat16), "col", scatter_dimension=0, tiled=True
        ).astype(jnp.float32),
        lax.psum_scatter(
            grad_cquery.astype(jnp.bfloat16), "col", scatter_dimension=0, tiled=True
        ).astype(jnp.float32),
        lax.psum_scatter(
            grad_ckey.astype(jnp.bfloat16), "col", scatter_dimension=0, tiled=True
        ).astype(jnp.float32),
        lax.psum_scatter(
            grad_cvalue.astype(jnp.bfloat16), "col", scatter_dimension=0, tiled=True
        ).astype(jnp.float32),
        lax.psum_scatter(
            grad_up.astype(jnp.bfloat16), "col", scatter_dimension=0, tiled=True
        ).astype(jnp.float32),
    )
    grad_out, grad_cout, grad_down = (
        lax.psum_scatter(
            grad_out.astype(jnp.bfloat16), "col", scatter_dimension=1, tiled=True
        ).astype(jnp.float32),
        lax.psum_scatter(
            grad_cout.astype(jnp.bfloat16), "col", scatter_dimension=1, tiled=True
        ).astype(jnp.float32),
        lax.psum_scatter(
            grad_down.astype(jnp.bfloat16), "col", scatter_dimension=1, tiled=True
        ).astype(jnp.float32),
    )
    summed = (
        lax.psum(grad_query.astype(jnp.bfloat16), "dp").astype(jnp.float32),
        lax.psum(grad_key.astype(jnp.bfloat16), "dp").astype(jnp.float32),
        lax.psum(grad_value.astype(jnp.bfloat16), "dp").astype(jnp.float32),
        lax.psum(grad_out.astype(jnp.bfloat16), "dp").astype(jnp.float32),
        lax.psum(grad_cquery.astype(jnp.bfloat16), "dp").astype(jnp.float32),
        lax.psum(grad_ckey.astype(jnp.bfloat16), "dp").astype(jnp.float32),
        lax.psum(grad_cvalue.astype(jnp.bfloat16), "dp").astype(jnp.float32),
        lax.psum(grad_cout.astype(jnp.bfloat16), "dp").astype(jnp.float32),
        lax.psum(grad_up.astype(jnp.bfloat16), "dp").astype(jnp.float32),
        lax.psum(grad_down.astype(jnp.bfloat16), "dp").astype(jnp.float32),
    )
    gains = lax.psum((self_gain, cross_gain, hidden_gain, final_gain), ("row", "col", "dp"))
    return (
        layer_out,
        grad_tokens,
        grad_encoded,
        gains[0],
        summed[0],
        summed[1],
        summed[2],
        summed[3],
        gains[1],
        summed[4],
        summed[5],
        summed[6],
        summed[7],
        gains[2],
        summed[8],
        summed[9],
        gains[3],
    )


def solution(mesh):
    return jax.shard_map(
        local,
        mesh=mesh,
        in_specs=(
            P(("dp", "col", "row"), None),
            P(("dp", "col", "row"), None),
            P(("dp", "col"), None),
            P(("dp", "col", "row"), None),
            P(),
            P("col", "row"),
            P("col", "row"),
            P("col", "row"),
            P("row", "col"),
            P(),
            P("col", "row"),
            P("col", "row"),
            P("col", "row"),
            P("row", "col"),
            P(),
            P("col", "row"),
            P("row", "col"),
            P(),
        ),
        out_specs=(
            P(("dp", "col", "row"), None),
            P(("dp", "col", "row"), None),
            P(("dp", "col", "row"), None),
            P(),
            P("col", "row"),
            P("col", "row"),
            P("col", "row"),
            P("row", "col"),
            P(),
            P("col", "row"),
            P("col", "row"),
            P("col", "row"),
            P("row", "col"),
            P(),
            P("col", "row"),
            P("row", "col"),
            P(),
        ),
        check_vma=False,
    )
```

profile of v0, /device:TPU:0, one launch (start us, length us, event | category | flops | bytes accessed | tf_op | source)
XLA Modules:
  0.0 1545.6 jit_solution(5854435203476800310)
XLA Ops:
  9.6 7.8 all_gather.40
  17.3 6.0 all_gather.41
  23.4 6.0 all_gather.42
  29.4 6.0 all_gather.43
  35.4 6.3 all-gather.7.cloned.1.call-done
  55.5 94.7 %while.64 = (s32[]{:T(128)}, bf16[4,512,192]{1,2,0:T(8,128)(2,1)S(1)}, f32[4,3,512]{2,1,0:T(4,128)S(1)}, s32[4]{0:T(128)S(1)}, s32[1,4]{1,0:T(1,128)S(1)}, /*ind...) while((s32[]{:T(128)}, ...), condition=%wide.region_6.7_spmd.clone.clone, body=%wide.region_2.6_spmd.clone.clone.sunk | while | flops 849493504 | bytes 44393620 | solution.py:91
  59.7 6.0 fusion.265
  65.8 6.8 fusion.266
  72.6 6.7 fusion.267
  83.5 6.0 fusion.265
  89.5 6.8 fusion.266
  96.2 6.7 fusion.267
  107.1 6.0 fusion.265
  113.1 6.8 fusion.266
  119.9 6.7 fusion.267
  130.8 6.0 fusion.265
  136.8 6.8 fusion.266
  143.6 6.7 fusion.267
  155.3 6.7 all_gather.44
  162.0 5.8 all_gather.46
  167.8 5.8 all_gather.47
  173.6 6.0 all_gather.48
  188.5 86.4 %all-reduce.12.cloned.1.call-done = f32[2048,768]{1,0:T(8,128)} async-done(((f32[2048,768]{1,0:T(8,128)}), f32[2048,768]{1,0:T(8,128)}) %all-reduce.12.cloned.1.call-update) | async-done | bytes 6291472 | tf_op jit(solution)/shard_map/psum | solution.py:183
  288.2 20.2 %while.63 = (s32[]{:T(128)}, bf16[4,512,192]{1,2,0:T(8,128)(2,1)S(1)}, f32[4,3,512]{2,1,0:T(4,128)S(1)}, bf16[4,512,3,64]{1,3,2,0:T(8,128)(2,1)S(1)}, bf16[1500,...) while((s32[]{:T(128)}, bf16[4,512,192]{1,2,0:T(8,128)(2,1)S(1)}, ...), condition=%wide.region_13.14_spmd, body=%wide.region_10.13_spmd.sunk | while | flops 610656768 | bytes 29655648 | solution.py:91
  314.9 118.3 %all-reduce.14.cloned.1.call-done = f32[2048,768]{1,0:T(8,128)} async-done(((f32[2048,768]{1,0:T(8,128)}), f32[2048,768]{1,0:T(8,128)}) %all-reduce.14.cloned.1.call-update) | async-done | bytes 6291472 | tf_op jit(solution)/shard_map/psum | solution.py:183
  433.2 5.3 fusion.142
  443.5 18.7 %multiply_convert_fusion.2 = (bf16[2048,768]{1,0:T(8,128)(2,1)}, f32[2048,768]{1,0:T(8,128)}, f32[2048,768]{1,0:T(8,128)}) fusion(bf16[2048,768]{1,0:T(8,128)(2,1)} %multiply_convert_fusion.3, bf16[768,768]{1,0:T(8,128)(2,1)} %all-gather.9.cloned.1.call-done), kind=kOutput, calls=%fused_computation.165 | convolution fusion | flops 2518155264 | bytes 20054016 | tf_op jit(solution)/shard_map/dot_general | solution.py:15
  462.1 7.5 fusion.146
  470.5 119.1 %all-reduce.16.cloned.1.call-done = f32[2048,768]{1,0:T(8,128)} async-done(((f32[2048,768]{1,0:T(8,128)}), f32[2048,768]{1,0:T(8,128)}) %all-reduce.16.cloned.1.call-update) | async-done | bytes 6291472 | tf_op jit(solution)/shard_map/psum | solution.py:183
  589.6 7.9 fusion.140
  597.5 22.3 %all-gather.13.cloned.1.call-done = bf16[2048,768]{1,0:T(8,128)(2,1)} async-done(((bf16[512,768]{1,0:T(8,128)(2,1)}), bf16[2048,768]{1,0:T(8,128)(2,1)}) %all-gather.13.cloned.1.call-update) | async-done | bytes 3145744 | tf_op jit(solution)/shard_map/all_gather | solution.py:169
  643.9 119.7 %all-reduce.18.cloned.1.call-done = f32[2048,768]{1,0:T(8,128)} async-done(((f32[2048,768]{1,0:T(8,128)}), f32[2048,768]{1,0:T(8,128)}) %all-reduce.18.cloned.1.call-update) | async-done | bytes 6291472 | tf_op jit(solution)/shard_map/psum | solution.py:183
  763.6 5.5 multiply_reduce_fusion.5
  786.2 110.7 %while.65 = (s32[]{:T(128)}, f32[1500,3,64]{0,2,1:T(8,128)S(1)}, f32[1500,3,64]{0,2,1:T(8,128)S(1)}, bf16[4,512,192]{1,2,0:T(8,128)(2,1)}, bf16[4,512,3,64]{1,3,...) while((s32[]{:T(128)}, f32[1500,3,64]{0,2,1:T(8,128)S(1)}, ...), condition=%wide.region_27.28_spmd.clone, body=%wide.region_25.27_spmd.clone.sunk | while | flops 1503843072 | bytes 135411952 | solution.py:134
  796.2 10.9 multiply_convert_fusion.8
  823.8 10.9 multiply_convert_fusion.8
  851.4 10.9 multiply_convert_fusion.8
  879.0 10.9 multiply_convert_fusion.8
  903.7 7.6 convolution_convert_fusion.8
  931.7 91.9 %all-reduce.20.cloned.1.call-done = f32[2048,768]{1,0:T(8,128)} async-done(((f32[2048,768]{1,0:T(8,128)}), f32[2048,768]{1,0:T(8,128)}) %all-reduce.20.cloned.1.call-update) | async-done | bytes 6291472 | tf_op jit(solution)/shard_map/psum | solution.py:183
  1023.6 5.5 multiply_reduce_fusion.4
  1030.0 6.1 fusion.137
  1050.2 141.9 %while.66 = (s32[]{:T(128)}, f32[2048,3,64]{0,2,1:T(8,128)}, f32[2048,3,64]{0,2,1:T(8,128)}, bf16[4,512,192]{1,2,0:T(8,128)(2,1)}, bf16[4,512,3,64]{1,3,2,0:T(8,...) while((s32[]{:T(128)}, f32[2048,3,64]{0,2,1:T(8,128)}, ...), condition=%wide.region_34.35_spmd.clone.clone, body=%wide.region_31.34_spmd.clone.clone.sunk | while | flops 2068954624 | bytes 147471712 | solution.py:134
  1063.1 5.8 multiply_reduce_fusion.24
  1068.9 6.1 multiply_convert_fusion.9
  1075.0 5.1 convolution_multiply_fusion.7
  1092.3 6.1 fusion.293
  1098.4 5.8 multiply_reduce_fusion.24
  1104.2 6.1 multiply_convert_fusion.9
  1110.3 5.1 convolution_multiply_fusion.7
  1128.2 6.1 fusion.293
  1134.3 5.8 multiply_reduce_fusion.24
  1140.1 6.1 multiply_convert_fusion.9
  1146.2 5.1 convolution_multiply_fusion.7
  1164.1 6.1 fusion.293
  1170.2 5.8 multiply_reduce_fusion.24
  1175.9 6.1 multiply_convert_fusion.9
  1207.5 6.6 convolution_convert_fusion.9
  1216.0 8.2 convert_element_type.265
  1244.0 22.8 %reduce-scatter.31.cloned.1.call-done = bf16[384,768]{1,0:T(8,128)(2,1)} async-done(((bf16[768,768]{1,0:T(8,128)(2,1)}), bf16[384,768]{1,0:T(8,128)(2,1)}) %reduce-scatter.31.cloned.1.call-update) | async-done | bytes 589840 | tf_op jit(solution)/shard_map/reduce_scatter | solution.py:286
  1288.5 25.8 %fusion.4 = bf16[376,768]{1,0:T(8,128)(2,1)} fusion(bf16[1500,768]{1,0:T(8,128)(2,1)} %add_convert_fusion.2), kind=kCustom, calls=%all-reduce-scatter | all-reduce-scatter fusion | flops 1155073 | bytes 2882048
  1327.8 37.6 %all-reduce.24.cloned.1.call-done = (bf16[384,192]{0,1:T(8,128)(2,1)}, bf16[384,192]{0,1:T(8,128)(2,1)}, bf16[384,192]{0,1:T(8,128)(2,1)}, bf16[192,384]{1,0:T(8...) async-done(((bf16[384,192]{0,1:T(8,128)(2,1)}, ...) | async-done | bytes 2359312 | tf_op jit(solution)/shard_map/psum | solution.py:302
  1382.9 103.1 %all-reduce.22.cloned.1.call-done = f32[2048,768]{1,0:T(8,128)} async-done(((f32[2048,768]{1,0:T(8,128)}), f32[2048,768]{1,0:T(8,128)}) %all-reduce.22.cloned.1.call-update) | async-done | bytes 6291472 | tf_op jit(solution)/shard_map/psum | solution.py:183
  1498.0 39.8 %all-reduce.2 = (f32[768]{0:T(1024)}, f32[768]{0:T(1024)}, f32[768]{0:T(1024)}, f32[768]{0:T(1024)}) all-reduce(f32[768]{0:T(1024)S(1)} %multiply_reduce_fusion.17, f32[768]{0:T(1024)S(1)} %multiply_reduce_fusion.15, f32[768]{0:T(1024)S(1)} %multiply_reduce_fusion.13, ...), channel_id=1, replica_groups=mesh['row'=4,'col'=2,'dp'=4] {'row','col','dp'}, use_global_device_ids=true, to_apply=%region_42.43 | all-reduce | flops 3072 | bytes 24576 | tf_op jit(solution)/shard_map/psum | solution.py:313
  (602 shorter events, 401.3 us)
Async XLA Ops:
  8.0 39.2 %copy-start.82 = (f32[768]{0:T(1024)S(1)}, f32[768]{0:T(1024)}, u32[]{:S(2)}) copy-start(f32[768]{0:T(1024)} %param.30) | copy-start | bytes 9220
  8.0 33.6 %all-gather.7.cloned.1.call-start = ((), (), s32[]{:S(2)}) async-start(), calls=%async_computation.10 | async-start | bytes 3932160 | tf_op jit(solution)/shard_map/all_gather | solution.py:169
  8.8 170.9 %all-gather.15.cloned.1.call-start = ((), (), s32[]{:S(2)}) async-start(), calls=%async_computation.21 | async-start | bytes 2887680 | tf_op jit(solution)/shard_map/all_gather | solution.py:169
  9.5 265.4 %all-reduce.12.cloned.1.call-start = ((), (), s32[]{:S(2)}) async-start(), calls=%async_computation.11 | async-start | bytes 12582912 | tf_op jit(solution)/shard_map/psum | solution.py:183
  17.3 33.6 %copy-start.48 = (bf16[768,192]{0,1:T(8,128)(2,1)}, bf16[768,192]{0,1:T(8,128)(2,1)S(1)}, u32[]{:S(2)}) copy-start(bf16[768,192]{0,1:T(8,128)(2,1)S(1)} %all_gather.40) | copy-start | bytes 884740
  23.4 26.3 %copy-start.50 = (bf16[768,192]{0,1:T(8,128)(2,1)}, bf16[768,192]{0,1:T(8,128)(2,1)S(1)}, u32[]{:S(2)}) copy-start(bf16[768,192]{0,1:T(8,128)(2,1)S(1)} %all_gather.41) | copy-start | bytes 884740
  29.4 19.1 %copy-start.55 = (bf16[768,192]{0,1:T(8,128)(2,1)}, bf16[768,192]{0,1:T(8,128)(2,1)S(1)}, u32[]{:S(2)}) copy-start(bf16[768,192]{0,1:T(8,128)(2,1)S(1)} %all_gather.42) | copy-start | bytes 884740
  35.4 115.0 %copy-start.43 = (bf16[192,768]{1,0:T(8,128)(2,1)}, bf16[192,768]{1,0:T(8,128)(2,1)S(1)}, u32[]{:S(2)}) copy-start(bf16[192,768]{1,0:T(8,128)(2,1)S(1)} %all_gather.43) | copy-start | bytes 884740
  150.3 29.3 %copy-start.37 = (bf16[4,512,3,64]{1,3,2,0:T(8,128)(2,1)}, bf16[4,512,3,64]{1,3,2,0:T(8,128)(2,1)S(1)}, u32[]{:S(2)}) copy-start(bf16[4,512,3,64]{1,3,2,0:T(8,128)(2,1)S(1)} %get-tuple-element.1281) | copy-start | bytes 2359300
  150.3 129.0 %copy-start.64 = (f32[4,3,512]{2,1,0:T(4,128)}, f32[4,3,512]{2,1,0:T(4,128)S(1)}, u32[]{:S(2)}) copy-start(f32[4,3,512]{2,1,0:T(4,128)S(1)} %get-tuple-element.1177) | copy-start | bytes 73732
  151.4 10.6 copy-start.66
  155.1 12.7 copy-start.67
  155.1 18.5 %copy-start.68 = (bf16[192,384]{1,0:T(8,128)(2,1)S(1)}, bf16[192,384]{1,0:T(8,128)(2,1)}, u32[]{:S(2)}) copy-start(bf16[192,384]{1,0:T(8,128)(2,1)} %param.39) | copy-start | bytes 442372
  155.2 278.0 %all-reduce.14.cloned.1.call-start = ((), (), s32[]{:S(2)}) async-start(), calls=%async_computation.12 | async-start | bytes 12582912 | tf_op jit(solution)/shard_map/psum | solution.py:183
  162.0 119.2 %copy-start.54 = (bf16[768,192]{0,1:T(8,128)(2,1)}, bf16[768,192]{0,1:T(8,128)(2,1)S(1)}, u32[]{:S(2)}) copy-start(bf16[768,192]{0,1:T(8,128)(2,1)S(1)} %all_gather.44) | copy-start | bytes 884740
  167.8 20.7 %copy-start.52 = (bf16[768,192]{0,1:T(8,128)(2,1)}, bf16[768,192]{0,1:T(8,128)(2,1)S(1)}, u32[]{:S(2)}) copy-start(bf16[768,192]{0,1:T(8,128)(2,1)S(1)} %all_gather.46) | copy-start | bytes 884740
  173.6 14.9 copy-start.57
  179.6 128.9 %copy-start.45 = (bf16[192,768]{1,0:T(8,128)(2,1)}, bf16[192,768]{1,0:T(8,128)(2,1)S(1)}, u32[]{:S(2)}) copy-start(bf16[192,768]{1,0:T(8,128)(2,1)S(1)} %all_gather.48) | copy-start | bytes 884740
  313.3 130.2 %all-gather.9.cloned.1.call-start = ((), (), s32[]{:S(2)}) async-start(), calls=%async_computation.13 | async-start | bytes 1769472 | tf_op jit(solution)/shard_map/all_gather | solution.py:195
  313.9 148.3 %all-gather.11.cloned.1.call-start = ((), (), s32[]{:S(2)}) async-start(), calls=%async_computation.14 | async-start | bytes 1769472 | tf_op jit(solution)/shard_map/all_gather | solution.py:200
  314.5 275.1 %all-reduce.16.cloned.1.call-start = ((), (), s32[]{:S(2)}) async-start(), calls=%async_computation.15 | async-start | bytes 12582912 | tf_op jit(solution)/shard_map/psum | solution.py:183
  469.6 150.1 %all-gather.13.cloned.1.call-start = ((), (), s32[]{:S(2)}) async-start(), calls=%async_computation.16 | async-start | bytes 3932160 | tf_op jit(solution)/shard_map/all_gather | solution.py:169
  470.2 149.5 %copy-start.80 = (f32[768]{0:T(1024)S(1)}, f32[768]{0:T(1024)}, u32[]{:S(2)}) copy-start(f32[768]{0:T(1024)} %param.43) | copy-start | bytes 9220
  470.2 293.3 %all-reduce.18.cloned.1.call-start = ((), (), s32[]{:S(2)}) async-start(), calls=%async_computation.17 | async-start | bytes 12582912 | tf_op jit(solution)/shard_map/psum | solution.py:183
  619.8 8.1 slice-start.10
  619.8 10.1 slice-start.12
  624.6 8.2 slice-start.13
  624.7 8.4 copy-start.91
  627.8 9.8 copy-start.22
  627.8 146.6 %copy-start.87 = (f32[2048]{0:T(1024)}, f32[2048]{0:T(1024)S(1)}, u32[]{:S(2)}) copy-start(f32[2048]{0:T(1024)S(1)} %negate_multiply_fusion.4) | copy-start | bytes 24580
  643.8 379.8 %all-reduce.20.cloned.1.call-start = ((), (), s32[]{:S(2)}) async-start(), calls=%async_computation.18 | async-start | bytes 12582912 | tf_op jit(solution)/shard_map/psum | solution.py:183
  763.6 10.9 slice-start.8
  778.0 8.2 copy-start.26
  903.6 324.5 %reduce-scatter.49.cloned.1.call-start = ((), (), s32[]{:S(2)}) async-start(), calls=%async_computation.30 | async-start | bytes 1769472
  914.0 316.3 %reduce-scatter.47.cloned.1.call-start = ((), (), s32[]{:S(2)}) async-start(), calls=%async_computation.29 | async-start | bytes 589824
  918.9 313.1 %reduce-scatter.41.cloned.1.call-start = ((), (), s32[]{:S(2)}) async-start(), calls=%async_computation.26 | async-start | bytes 589824
  923.2 310.5 %reduce-scatter.43.cloned.1.call-start = ((), (), s32[]{:S(2)}) async-start(), calls=%async_computation.27 | async-start | bytes 589824
  923.3 100.3 %copy-start.62 = (f32[2048]{0:T(1024)S(1)}, f32[2048]{0:T(1024)}, u32[]{:S(2)}) copy-start(f32[2048]{0:T(1024)} %copy-done.61) | copy-start | bytes 24580
  923.4 100.2 %copy-start.86 = (f32[768]{0:T(1024)S(1)}, f32[768]{0:T(1024)}, u32[]{:S(2)}) copy-start(f32[768]{0:T(1024)} %param.35) | copy-start | bytes 9220
  927.4 308.0 %reduce-scatter.45.cloned.1.call-start = ((), (), s32[]{:S(2)}) async-start(), calls=%async_computation.28 | async-start | bytes 589824
  931.6 97.5 %copy-start.74 = (f32[2048]{0:T(1024)S(1)}, f32[2048]{0:T(1024)}, u32[]{:S(2)}) copy-start(f32[2048]{0:T(1024)} %copy-done.73) | copy-start | bytes 24580
  931.6 97.5 %copy-start.76 = (f32[2048]{0:T(1024)S(1)}, f32[2048]{0:T(1024)}, u32[]{:S(2)}) copy-start(f32[2048]{0:T(1024)} %copy-done.75) | copy-start | bytes 24580
  931.7 305.5 %reduce-scatter.39.cloned.1.call-start = ((), (), s32[]{:S(2)}) async-start(), calls=%async_computation.25 | async-start | bytes 589824
  1023.6 12.5 slice-start.4
  1049.2 189.6 %reduce-scatter.33.cloned.1.call-start = ((), (), s32[]{:S(2)}) async-start(), calls=%async_computation.22 | async-start | bytes 589824
  1198.0 42.5 %reduce-scatter.35.cloned.1.call-start = ((), (), s32[]{:S(2)}) async-start(), calls=%async_computation.23 | async-start | bytes 589824
  1203.1 39.2 %reduce-scatter.37.cloned.1.call-start = ((), (), s32[]{:S(2)}) async-start(), calls=%async_computation.24 | async-start | bytes 589824
  1206.5 9.0 copy-start.7
  1207.4 59.4 %reduce-scatter.31.cloned.1.call-start = ((), (), s32[]{:S(2)}) async-start(), calls=%async_computation.20 | async-start | bytes 1769472 | tf_op jit(solution)/shard_map/reduce_scatter | solution.py:286
  1214.1 151.3 %all-reduce.24.cloned.1.call-start = ((), (), s32[]{:S(2)}) async-start(), calls=%async_computation.31 | async-start | bytes 4718592 | tf_op jit(solution)/shard_map/psum | solution.py:302
  1215.4 9.2 slice-start
  1215.5 9.7 slice-start.2
  1216.0 8.7 copy-start.23
  1216.0 8.8 slice-start.1
  1216.0 9.7 slice-start.3
  1216.0 10.9 slice-start.6
  1227.6 42.4 %copy-start.81 = (f32[768]{0:T(1024)S(1)}, f32[768]{0:T(1024)}, u32[]{:S(2)}) copy-start(f32[768]{0:T(1024)} %param.43) | copy-start | bytes 9220
  1228.1 44.6 %copy-start.53 = (bf16[768,192]{0,1:T(8,128)(2,1)S(1)}, bf16[768,192]{0,1:T(8,128)(2,1)}, u32[]{:S(2)}) copy-start(bf16[768,192]{0,1:T(8,128)(2,1)} %copy-done.52) | copy-start | bytes 884740
  1266.8 219.2 %all-reduce.22.cloned.1.call-start = ((), (), s32[]{:S(2)}) async-start(), calls=%async_computation.19 | async-start | bytes 12582912 | tf_op jit(solution)/shard_map/psum | solution.py:183
  1315.0 3.5 collective-permute-start
  1318.4 167.6 %copy-start.60 = (f32[2048]{0:T(1024)S(1)}, f32[2048]{0:T(1024)}, u32[]{:S(2)}) copy-start(f32[2048]{0:T(1024)} %copy-done.59) | copy-start | bytes 24580
  1318.5 167.6 %copy-start.83 = (f32[768]{0:T(1024)S(1)}, f32[768]{0:T(1024)}, u32[]{:S(2)}) copy-start(f32[768]{0:T(1024)} %param.30) | copy-start | bytes 9220
  1378.6 111.3 %copy-start.72 = (f32[2048]{0:T(1024)S(1)}, f32[2048]{0:T(1024)}, u32[]{:S(2)}) copy-start(f32[2048]{0:T(1024)} %copy-done.71) | copy-start | bytes 24580
  1378.6 111.3 %copy-start.70 = (f32[2048]{0:T(1024)S(1)}, f32[2048]{0:T(1024)}, u32[]{:S(2)}) copy-start(f32[2048]{0:T(1024)} %copy-done.69) | copy-start | bytes 24580
  (92 other events, 380.2 us)
Sparse Core Ops, SparseCore 0:
  10.4 31.2 all-gather.6
  43.2 23.7 all-gather.14
  155.3 119.5 all-reduce.11
  313.4 119.7 all-reduce.13
  469.8 119.7 all-reduce.15
  591.0 28.7 all-gather.12
  643.9 119.5 all-reduce.17
  903.8 119.7 all-reduce.19
Sparse Core Ops, SparseCore 1:
  315.3 22.8 all-gather.8
  339.6 22.6 all-gather.10
  914.1 22.0 reduce-scatter.48
  938.4 13.1 reduce-scatter.46
  953.9 13.1 reduce-scatter.40
  969.3 13.1 reduce-scatter.42
  984.6 13.1 reduce-scatter.44
  1049.3 13.3 reduce-scatter.38
  1198.1 13.3 reduce-scatter.32
  1213.8 13.1 reduce-scatter.34
  1229.0 13.1 reduce-scatter.36
  1245.0 21.7 reduce-scatter.30
  1270.5 94.9 all-reduce.23
  1367.8 118.2 all-reduce.21
where the time goes:
time: 1550 us
  waiting for transfers between devices  731 us (47%)
  matrix products  331 us (21%)
  other arithmetic  244 us (16%)
  blocking collectives  116 us (7%)
  local copies, waits for them, and re-layouts  101 us (7%)
  between operations  18.4 us (1%)
    psum x6, waiting for transfers between devices, settle(): return lax.psum(apply(parts), 'row')  638 us
    unnamed x227, local copies, waits for them, and re-layouts  69.1 us
    convert_element_type x8, other arithmetic, one_block(): sloped = (weights * (through - centre)).astype(jnp.bfloat16)  68 us
    dot_general x16, matrix products, block_scores(): jnp.einsum('qhd,khd->hqk', piece, split_k, preferred_element_type=jnp.flo...  51.3 us
    dot_general x10, matrix products, matmul(): return jnp.dot(left, right, preferred_element_type=jnp.float32)  45.2 us
    dot_general x8, matrix products, one_block(): jnp.einsum('qhd,khd->hqk', grad_piece, split_v, preferred_element_type=jn...  42.6 us
    psum x1, blocking collectives, local(): lax.psum((self_gain, cross_gain, hidden_gain, final_gain), ('row', 'col',...  39.8 us
    psum x1, waiting for transfers between devices, local(): lax.psum(grad_query.astype(jnp.bfloat16), 'dp').astype(jnp.float32)  37.6 us
  transfers between devices with their start and end apart: 23, of which 10 were waited for; matrix products, arithmetic and copies ran while one was open for 30% of the time, Pallas kernels for 0%

commit v1 on v0

--- a/solution.py
+++ b/solution.py
@@ -180,7 +180,7 @@
         ).astype(jnp.float32)
 
     def settle(parts, apply):
-        return lax.psum(apply(parts), "row")
+        return jnp.sum(lax.all_gather(apply(parts), "row"), axis=0)
 
     def gain_term(upstream, rows_in):
         return jnp.sum(own_slice(upstream) * unit_rows(own_slice(rows_in)), axis=0)

time: 1550 us -> 1840 us (1.19)
  waiting for transfers between devices: 731 us -> 940 us
  other arithmetic: 244 us -> 320 us
    all_gather x0 -> x6, waiting for transfers between devices: none -> 845 us  [settle(): return jnp.sum(lax.all_gather(apply(parts), 'row'), axis=0)]
    psum x6 -> x0, waiting for transfers between devices: 638 us -> none  [settle(): return lax.psum(apply(parts), 'row')]
    reduce_sum x0 -> x6, other arithmetic: none -> 76.8 us  [settle(): return jnp.sum(lax.all_gather(apply(parts), 'row'), axis=0)]
    unnamed x227 -> x235, local copies, waits for them, and re-layouts: 69.1 us -> 63.4 us
  transfers between devices with their start and end apart: 23 -> 23, of which waited for: 10 -> 13; matrix products, arithmetic and copies ran while one was open for 30% -> 28% of each run, Pallas kernels for 0% -> 0%
where the time goes in v1:
time: 1840 us; the launch traced here: 1820 us
  waiting for transfers between devices  940 us (51%)
  matrix products  331 us (18%)
  other arithmetic  320 us (17%)
  blocking collectives  115 us (6%)
  local copies, waits for them, and re-layouts  95.5 us (5%)
    all_gather x6, waiting for transfers between devices, settle(): return jnp.sum(lax.all_gather(apply(parts), 'row'), axis=0)  845 us
    reduce_sum x6, other arithmetic, settle(): return jnp.sum(lax.all_gather(apply(parts), 'row'), axis=0)  76.8 us
    convert_element_type x8, other arithmetic, one_block(): sloped = (weights * (through - centre)).astype(jnp.bfloat16)  68.4 us
    unnamed x235, local copies, waits for them, and re-layouts  63.4 us
    dot_general x16, matrix products, block_scores(): jnp.einsum('qhd,khd->hqk', piece, split_k, preferred_element_type=jnp.flo...  51.3 us
    dot_general x10, matrix products, matmul(): return jnp.dot(left, right, preferred_element_type=jnp.float32)  45.9 us
    dot_general x8, matrix products, one_block(): jnp.einsum('qhd,khd->hqk', grad_piece, split_v, preferred_element_type=jn...  42.6 us
    psum x1, blocking collectives, local(): lax.psum((self_gain, cross_gain, hidden_gain, final_gain), ('row', 'col',...  39.5 us
  transfers between devices with their start and end apart: 23, of which 13 were waited for; matrix products, arithmetic and copies ran while one was open for 28% of the time, Pallas kernels for 0%

profile of v1, /device:TPU:0, one launch (start us, length us, event | category | flops | bytes accessed | tf_op | source)
XLA Modules:
  0.0 1824.0 jit_solution(8895228092244819178)
XLA Ops:
  8.7 7.8 all_gather.76
  16.5 6.0 all_gather.77
  22.5 6.0 all_gather.78
  28.5 6.0 all_gather.79
  34.6 6.3 all-gather.19.cloned.1.call-done
  54.5 94.8 %while.64 = (s32[]{:T(128)}, bf16[4,512,192]{1,2,0:T(8,128)(2,1)S(1)}, f32[4,3,512]{2,1,0:T(4,128)S(1)}, s32[4]{0:T(128)S(1)}, s32[1,4]{1,0:T(1,128)S(1)}, /*ind...) while((s32[]{:T(128)}, ...), condition=%wide.region_6.7_spmd.clone.clone, body=%wide.region_2.6_spmd.clone.clone.sunk | while | flops 849493504 | bytes 44393620 | solution.py:91
  58.7 6.1 fusion.265
  64.8 6.8 fusion.266
  71.5 6.7 fusion.267
  82.4 6.0 fusion.265
  88.5 6.8 fusion.266
  95.2 6.7 fusion.267
  106.1 6.0 fusion.265
  112.1 6.8 fusion.266
  118.9 6.7 fusion.267
  129.8 6.0 fusion.265
  135.8 6.8 fusion.266
  142.6 6.7 fusion.267
  154.3 6.7 all_gather.82
  161.1 5.8 all_gather.84
  166.9 5.8 all_gather.85
  172.7 6.0 all_gather.86
  187.5 121.7 %all-gather.27.cloned.1.call-done = f32[8192,768]{1,0:T(8,128)} async-done(((f32[2048,768]{1,0:T(8,128)}), f32[8192,768]{1,0:T(8,128)}) %all-gather.27.cloned.1.call-update) | async-done | bytes 25165840 | tf_op jit(solution)/shard_map/all_gather | solution.py:183
  309.2 12.7 reduce_sum.386
  335.3 20.2 %while.63 = (s32[]{:T(128)}, bf16[4,512,192]{1,2,0:T(8,128)(2,1)S(1)}, f32[4,3,512]{2,1,0:T(4,128)S(1)}, bf16[4,512,3,64]{1,3,2,0:T(8,128)(2,1)S(1)}, bf16[1500,...) while((s32[]{:T(128)}, bf16[4,512,192]{1,2,0:T(8,128)(2,1)S(1)}, ...), condition=%wide.region_13.14_spmd, body=%wide.region_10.13_spmd.sunk | while | flops 610656768 | bytes 29655648 | solution.py:91
  362.1 153.3 %all-gather.29.cloned.1.call-done = f32[8192,768]{1,0:T(8,128)} async-done(((f32[2048,768]{1,0:T(8,128)}), f32[8192,768]{1,0:T(8,128)}) %all-gather.29.cloned.1.call-update) | async-done | bytes 25165840 | tf_op jit(solution)/shard_map/all_gather | solution.py:183
  515.4 13.0 reduce_sum.392
  539.6 19.2 %multiply_convert_fusion.2 = (bf16[2048,768]{1,0:T(8,128)(2,1)}, f32[2048,768]{1,0:T(8,128)}, f32[2048,768]{1,0:T(8,128)}) fusion(bf16[2048,768]{1,0:T(8,128)(2,1)S(1)} %multiply_convert_fusion.3, bf16[768,768]{1,0:T(8,128)(2,1)} %all-gather.21.cloned.1.call-done), kind=kOutput, calls=%fused_computation.165 | convolution fusion | flops 2518155264 | bytes 20054016 | tf_op jit(solution)/shard_map/dot_general | solution.py:15
  563.8 7.7 fusion.146
  572.5 154.0 %all-gather.31.cloned.1.call-done = f32[8192,768]{1,0:T(8,128)} async-done(((f32[2048,768]{1,0:T(8,128)}), f32[8192,768]{1,0:T(8,128)}) %all-gather.31.cloned.1.call-update) | async-done | bytes 25165840 | tf_op jit(solution)/shard_map/all_gather | solution.py:183
  726.4 12.9 reduce_sum.448
  739.4 7.9 fusion.140
  747.3 9.2 all-gather.25.cloned.1.call-done
  766.0 7.1 add_convert_fusion
  779.4 154.9 %all-gather.33.cloned.1.call-done = f32[8192,768]{1,0:T(8,128)} async-done(((f32[2048,768]{1,0:T(8,128)}), f32[8192,768]{1,0:T(8,128)}) %all-gather.33.cloned.1.call-update) | async-done | bytes 25165840 | tf_op jit(solution)/shard_map/all_gather | solution.py:183
  934.3 12.6 reduce_sum.453
  969.5 110.9 %while.65 = (s32[]{:T(128)}, f32[1500,3,64]{0,2,1:T(8,128)S(1)}, f32[1500,3,64]{0,2,1:T(8,128)S(1)}, bf16[4,512,192]{1,2,0:T(8,128)(2,1)}, bf16[4,512,3,64]{1,3,...) while((s32[]{:T(128)}, f32[1500,3,64]{0,2,1:T(8,128)S(1)}, ...), condition=%wide.region_27.28_spmd.clone, body=%wide.region_25.27_spmd.clone.sunk | while | flops 1503843072 | bytes 135411952 | solution.py:134
  979.5 11.0 multiply_convert_fusion.8
  1007.2 11.0 multiply_convert_fusion.8
  1034.9 11.0 multiply_convert_fusion.8
  1062.6 11.0 multiply_convert_fusion.8
  1087.2 7.6 convolution_convert_fusion.8
  1117.9 124.3 %all-gather.35.cloned.1.call-done = f32[8192,768]{1,0:T(8,128)} async-done(((f32[2048,768]{1,0:T(8,128)}), f32[8192,768]{1,0:T(8,128)}) %all-gather.35.cloned.1.call-update) | async-done | bytes 25165840 | tf_op jit(solution)/shard_map/all_gather | solution.py:183
  1242.1 13.0 reduce_sum.456
  1261.7 6.0 fusion.137
  1281.8 142.4 %while.66 = (s32[]{:T(128)}, f32[2048,3,64]{0,2,1:T(8,128)}, f32[2048,3,64]{0,2,1:T(8,128)}, bf16[4,512,192]{1,2,0:T(8,128)(2,1)}, bf16[4,512,3,64]{1,3,2,0:T(8,...) while((s32[]{:T(128)}, f32[2048,3,64]{0,2,1:T(8,128)}, ...), condition=%wide.region_34.35_spmd.clone.clone, body=%wide.region_31.34_spmd.clone.clone.sunk | while | flops 2068954624 | bytes 147471712 | solution.py:134
  1294.8 5.8 multiply_reduce_fusion.24
  1300.6 6.1 multiply_convert_fusion.9
  1324.0 6.2 fusion.293
  1336.0 6.1 multiply_convert_fusion.9
  1360.1 6.2 fusion.293
  1372.0 6.1 multiply_convert_fusion.9
  1396.0 6.2 fusion.293
  1402.2 5.8 multiply_reduce_fusion.24
  1408.0 6.1 multiply_convert_fusion.9
  1439.6 6.6 convolution_convert_fusion.9
  1460.4 13.7 reduce-scatter.37.cloned.1.call-done
  1475.8 22.8 %reduce-scatter.31.cloned.1.call-done = bf16[384,768]{1,0:T(8,128)(2,1)} async-done(((bf16[768,768]{1,0:T(8,128)(2,1)}), bf16[384,768]{1,0:T(8,128)(2,1)}) %reduce-scatter.31.cloned.1.call-update) | async-done | bytes 589840 | tf_op jit(solution)/shard_map/reduce_scatter | solution.py:286
  1507.2 8.2 convert_element_type.265
  1525.0 25.6 %fusion.4 = bf16[376,768]{1,0:T(8,128)(2,1)} fusion(bf16[1500,768]{1,0:T(8,128)(2,1)} %add_convert_fusion.2), kind=kCustom, calls=%all-reduce-scatter | all-reduce-scatter fusion | flops 1155073 | bytes 2882048
  1565.6 31.9 %all-reduce.6.cloned.1.call-done = (bf16[384,192]{0,1:T(8,128)(2,1)}, bf16[384,192]{0,1:T(8,128)(2,1)}, bf16[384,192]{0,1:T(8,128)(2,1)}, bf16[192,384]{1,0:T(8,...) async-done(((bf16[384,192]{0,1:T(8,128)(2,1)}, ...) | async-done | bytes 2359312 | tf_op jit(solution)/shard_map/psum | solution.py:302
  1615.4 137.3 %all-gather.37.cloned.1.call-done = f32[8192,768]{1,0:T(8,128)} async-done(((f32[2048,768]{1,0:T(8,128)}), f32[8192,768]{1,0:T(8,128)}) %all-gather.37.cloned.1.call-update) | async-done | bytes 25165840 | tf_op jit(solution)/shard_map/all_gather | solution.py:183
  1752.7 12.6 reduce_sum.459
  1777.2 39.5 %all-reduce.2 = (f32[768]{0:T(1024)}, f32[768]{0:T(1024)}, f32[768]{0:T(1024)}, f32[768]{0:T(1024)}) all-reduce(f32[768]{0:T(1024)S(1)} %multiply_reduce_fusion.17, f32[768]{0:T(1024)S(1)} %multiply_reduce_fusion.15, f32[768]{0:T(1024)S(1)} %get-tuple-element.857, ...), channel_id=1, replica_groups=mesh['row'=4,'col'=2,'dp'=4] {'row','col','dp'}, use_global_device_ids=true, to_apply=%region_42.43 | all-reduce | flops 3072 | bytes 24576 | tf_op jit(solution)/shard_map/psum | solution.py:313
  (615 shorter events, 437.6 us)
Async XLA Ops:
  7.2 39.2 %copy-start.86 = (f32[768]{0:T(1024)S(1)}, f32[768]{0:T(1024)}, u32[]{:S(2)}) copy-start(f32[768]{0:T(1024)} %param.30) | copy-start | bytes 9220
  7.2 33.6 %all-gather.19.cloned.1.call-start = ((), (), s32[]{:S(2)}) async-start(), calls=%async_computation.10 | async-start | bytes 3932160 | tf_op jit(solution)/shard_map/all_gather | solution.py:169
  7.9 170.8 %all-gather.39.cloned.1.call-start = ((), (), s32[]{:S(2)}) async-start(), calls=%async_computation.21 | async-start | bytes 2887680 | tf_op jit(solution)/shard_map/all_gather | solution.py:169
  8.7 300.5 %all-gather.27.cloned.1.call-start = ((), (), s32[]{:S(2)}) async-start(), calls=%async_computation.15 | async-start | bytes 31457280 | tf_op jit(solution)/shard_map/all_gather | solution.py:183
  16.5 33.4 %copy-start.52 = (bf16[768,192]{0,1:T(8,128)(2,1)}, bf16[768,192]{0,1:T(8,128)(2,1)S(1)}, u32[]{:S(2)}) copy-start(bf16[768,192]{0,1:T(8,128)(2,1)S(1)} %all_gather.76) | copy-start | bytes 884740
  22.5 26.2 %copy-start.54 = (bf16[768,192]{0,1:T(8,128)(2,1)}, bf16[768,192]{0,1:T(8,128)(2,1)S(1)}, u32[]{:S(2)}) copy-start(bf16[768,192]{0,1:T(8,128)(2,1)S(1)} %all_gather.77) | copy-start | bytes 884740
  28.5 19.0 %copy-start.59 = (bf16[768,192]{0,1:T(8,128)(2,1)}, bf16[768,192]{0,1:T(8,128)(2,1)S(1)}, u32[]{:S(2)}) copy-start(bf16[768,192]{0,1:T(8,128)(2,1)S(1)} %all_gather.78) | copy-start | bytes 884740
  34.6 114.9 %copy-start.46 = (bf16[192,768]{1,0:T(8,128)(2,1)}, bf16[192,768]{1,0:T(8,128)(2,1)S(1)}, u32[]{:S(2)}) copy-start(bf16[192,768]{1,0:T(8,128)(2,1)S(1)} %all_gather.79) | copy-start | bytes 884740
  149.3 29.4 %copy-start.38 = (bf16[4,512,3,64]{1,3,2,0:T(8,128)(2,1)}, bf16[4,512,3,64]{1,3,2,0:T(8,128)(2,1)S(1)}, u32[]{:S(2)}) copy-start(bf16[4,512,3,64]{1,3,2,0:T(8,128)(2,1)S(1)} %get-tuple-element.1286) | copy-start | bytes 2359300
  149.3 172.5 %copy-start.68 = (f32[4,3,512]{2,1,0:T(4,128)}, f32[4,3,512]{2,1,0:T(4,128)S(1)}, u32[]{:S(2)}) copy-start(f32[4,3,512]{2,1,0:T(4,128)S(1)} %get-tuple-element.1179) | copy-start | bytes 73732
  150.5 10.6 copy-start.70
  154.2 12.7 copy-start.71
  154.2 18.5 %copy-start.72 = (bf16[192,384]{1,0:T(8,128)(2,1)S(1)}, bf16[192,384]{1,0:T(8,128)(2,1)}, u32[]{:S(2)}) copy-start(bf16[192,384]{1,0:T(8,128)(2,1)} %param.39) | copy-start | bytes 442372
  154.3 361.2 %all-gather.29.cloned.1.call-start = ((), (), s32[]{:S(2)}) async-start(), calls=%async_computation.16 | async-start | bytes 31457280 | tf_op jit(solution)/shard_map/all_gather | solution.py:183
  161.1 167.2 %copy-start.58 = (bf16[768,192]{0,1:T(8,128)(2,1)}, bf16[768,192]{0,1:T(8,128)(2,1)S(1)}, u32[]{:S(2)}) copy-start(bf16[768,192]{0,1:T(8,128)(2,1)S(1)} %all_gather.82) | copy-start | bytes 884740
  166.9 20.6 %copy-start.56 = (bf16[768,192]{0,1:T(8,128)(2,1)}, bf16[768,192]{0,1:T(8,128)(2,1)S(1)}, u32[]{:S(2)}) copy-start(bf16[768,192]{0,1:T(8,128)(2,1)S(1)} %all_gather.84) | copy-start | bytes 884740
  172.7 14.8 copy-start.61
  178.7 177.0 %copy-start.48 = (bf16[192,768]{1,0:T(8,128)(2,1)}, bf16[192,768]{1,0:T(8,128)(2,1)S(1)}, u32[]{:S(2)}) copy-start(bf16[192,768]{1,0:T(8,128)(2,1)S(1)} %all_gather.86) | copy-start | bytes 884740
  355.6 172.8 %copy-start.67 = (f32[4,3,512]{2,1,0:T(4,128)}, f32[4,3,512]{2,1,0:T(4,128)S(1)}, u32[]{:S(2)}) copy-start(f32[4,3,512]{2,1,0:T(4,128)S(1)} %get-tuple-element.1144) | copy-start | bytes 73732
  360.5 179.1 %all-gather.21.cloned.1.call-start = ((), (), s32[]{:S(2)}) async-start(), calls=%async_computation.11 | async-start | bytes 1769472 | tf_op jit(solution)/shard_map/all_gather | solution.py:195
  361.1 202.7 %all-gather.23.cloned.1.call-start = ((), (), s32[]{:S(2)}) async-start(), calls=%async_computation.12 | async-start | bytes 1769472 | tf_op jit(solution)/shard_map/all_gather | solution.py:200
  361.7 364.8 %all-gather.31.cloned.1.call-start = ((), (), s32[]{:S(2)}) async-start(), calls=%async_computation.17 | async-start | bytes 31457280 | tf_op jit(solution)/shard_map/all_gather | solution.py:183
  537.4 21.4 %copy-start.45 = (bf16[2048,768]{1,0:T(8,128)(2,1)}, bf16[2048,768]{1,0:T(8,128)(2,1)S(1)}, u32[]{:S(2)}) copy-start(bf16[2048,768]{1,0:T(8,128)(2,1)S(1)} %multiply_convert_fusion.3) | copy-start | bytes 9437188
  571.5 185.0 %all-gather.25.cloned.1.call-start = ((), (), s32[]{:S(2)}) async-start(), calls=%async_computation.13 | async-start | bytes 3932160 | tf_op jit(solution)/shard_map/all_gather | solution.py:169
  572.3 362.0 %all-gather.33.cloned.1.call-start = ((), (), s32[]{:S(2)}) async-start(), calls=%async_computation.18 | async-start | bytes 31457280 | tf_op jit(solution)/shard_map/all_gather | solution.py:183
  739.4 17.2 copy-start.84
  756.5 8.1 slice-start.12
  764.6 8.5 copy-start.23
  764.6 193.2 %copy-start.91 = (f32[2048]{0:T(1024)}, f32[2048]{0:T(1024)S(1)}, u32[]{:S(2)}) copy-start(f32[2048]{0:T(1024)S(1)} %negate_multiply_fusion.4) | copy-start | bytes 24580
  765.9 8.9 copy-start.94
  779.4 462.8 %all-gather.35.cloned.1.call-start = ((), (), s32[]{:S(2)}) async-start(), calls=%async_computation.19 | async-start | bytes 31457280 | tf_op jit(solution)/shard_map/all_gather | solution.py:183
  946.9 10.9 slice-start.10
  961.4 8.2 copy-start.7
  961.4 8.2 copy-start.27
  1087.2 359.1 %reduce-scatter.49.cloned.1.call-start = ((), (), s32[]{:S(2)}) async-start(), calls=%async_computation.30 | async-start | bytes 1769472
  1097.8 350.6 %reduce-scatter.47.cloned.1.call-start = ((), (), s32[]{:S(2)}) async-start(), calls=%async_computation.29 | async-start | bytes 589824
  1104.1 346.0 %reduce-scatter.41.cloned.1.call-start = ((), (), s32[]{:S(2)}) async-start(), calls=%async_computation.26 | async-start | bytes 589824
  1109.2 342.7 %reduce-scatter.43.cloned.1.call-start = ((), (), s32[]{:S(2)}) async-start(), calls=%async_computation.27 | async-start | bytes 589824
  1113.6 340.0 %reduce-scatter.45.cloned.1.call-start = ((), (), s32[]{:S(2)}) async-start(), calls=%async_computation.28 | async-start | bytes 589824
  1117.8 337.5 %reduce-scatter.39.cloned.1.call-start = ((), (), s32[]{:S(2)}) async-start(), calls=%async_computation.25 | async-start | bytes 589824
  1242.1 13.0 copy-start.66
  1242.1 13.0 copy-start.90
  1255.2 12.6 slice-start.4
  1280.8 176.1 %reduce-scatter.33.cloned.1.call-start = ((), (), s32[]{:S(2)}) async-start(), calls=%async_computation.22 | async-start | bytes 589824
  1282.0 8.0 copy-start.43
  1316.1 8.0 copy-start.43
  1352.1 8.0 copy-start.43
  1388.1 8.0 copy-start.43
  1430.1 28.6 %reduce-scatter.35.cloned.1.call-start = ((), (), s32[]{:S(2)}) async-start(), calls=%async_computation.23 | async-start | bytes 589824
  1435.2 38.9 %reduce-scatter.37.cloned.1.call-start = ((), (), s32[]{:S(2)}) async-start(), calls=%async_computation.24 | async-start | bytes 589824
  1439.5 59.2 %copy-start.37 = (bf16[2048,3,64]{0,2,1:T(8,128)(2,1)S(1)}, bf16[2048,3,64]{0,2,1:T(8,128)(2,1)}, u32[]{:S(2)}) copy-start(bf16[2048,3,64]{0,2,1:T(8,128)(2,1)} %copy-done.36) | copy-start | bytes 2359300
  1439.5 59.2 %copy-start.55 = (bf16[768,192]{0,1:T(8,128)(2,1)S(1)}, bf16[768,192]{0,1:T(8,128)(2,1)}, u32[]{:S(2)}) copy-start(bf16[768,192]{0,1:T(8,128)(2,1)} %copy-done.54) | copy-start | bytes 884740
  1439.5 59.1 %reduce-scatter.31.cloned.1.call-start = ((), (), s32[]{:S(2)}) async-start(), calls=%async_computation.14 | async-start | bytes 1769472 | tf_op jit(solution)/shard_map/reduce_scatter | solution.py:286
  1446.2 151.3 %all-reduce.6.cloned.1.call-start = ((), (), s32[]{:S(2)}) async-start(), calls=%async_computation.31 | async-start | bytes 4718592 | tf_op jit(solution)/shard_map/psum | solution.py:302
  1498.6 254.0 %all-gather.37.cloned.1.call-start = ((), (), s32[]{:S(2)}) async-start(), calls=%async_computation.20 | async-start | bytes 31457280 | tf_op jit(solution)/shard_map/all_gather | solution.py:183
  1506.6 9.3 slice-start
  1506.6 9.8 slice-start.2
  1507.1 8.7 copy-start.24
  1507.1 8.8 slice-start.1
  1507.1 9.7 slice-start.3
  1507.2 11.5 slice-start.8
  1551.3 5.0 collective-permute-start
  1752.7 14.9 copy-start.64
  1752.7 15.0 copy-start.87
  (96 other events, 377.0 us)
Sparse Core Ops, SparseCore 0:
  9.6 31.2 all-gather.18
  42.4 23.7 all-gather.38
  154.4 154.7 all-gather.26
  360.6 154.7 all-gather.28
  516.8 22.7 all-gather.20
  541.0 22.7 all-gather.22
  571.6 154.7 all-gather.30
  728.0 28.4 all-gather.24
  779.5 154.7 all-gather.32
  1087.3 154.7 all-gather.34
  1245.0 21.8 reduce-scatter.48
  1268.9 13.1 reduce-scatter.46
  1284.4 13.1 reduce-scatter.40
  1299.7 13.1 reduce-scatter.42
  1315.0 13.1 reduce-scatter.44
  1330.4 13.1 reduce-scatter.38
  1430.2 13.0 reduce-scatter.32
  1445.4 13.1 reduce-scatter.34
  1460.9 13.1 reduce-scatter.36
  1476.7 21.8 reduce-scatter.30
  1502.4 95.0 all-reduce.5
  1599.1 153.5 all-gather.36
